TPU v7x, 32 devices: a whole 2x2x4 slice. The times are simulated.
32 devices in a mesh: rows: 8 (over z, x), cols: 4 (over y, core).
Axes of the slice: x: 2, y: 2, z: 4, core: 2. Of those that a mesh axis runs over, the one named last changes fastest.
Arguments:
- matrix: float32 [512, 32, 2, 128], P('rows', 'cols'), may hold values from -54 to 54
- plan: int32 [2, 4, 256], replicated, may hold values from 0 to 255, as said below
Outputs:
- rotated: float32 [512, 32, 2, 128], P('rows', 'cols')
Inputs may be any that keep to these rules, and one draw needn't show every extreme that they name: Each plan[s, r] pairs the 256 columns: partner of partner of i is i, and no column is its own partner.
All inputs are finite; a program needn't handle non-finite values.
Results may differ from a plain program's by a relative error of at most 0.0003.
Values sent between devices are 32-bit elements; how exact they have to be, the bound alone decides.
A program may use at most 128 MiB of HBM per device.

v0:
```python
import functools

import jax
import jax.numpy as jnp
from jax import lax
from jax.experimental import pallas as pl
from jax.experimental.pallas import tpu as pltpu
from jax.sharding import PartitionSpec as P

MESH = pl.DeviceIdType.MESH
NN = (((1,), (0,)), ((), ()))
NT = (((1,), (1,)), ((), ()))
F32 = jnp.float32
BF16 = jnp.bfloat16


def dot(a, b, dims=NN, precision=None):
    return lax.dot_general(a, b, dims, precision=precision, preferred_element_type=F32)


def exact_dot(a, b, dims=NN):
    return dot(a, b, dims, lax.Precision.HIGHEST)


def split(a):
    hi = a.astype(BF16)
    rest = a - hi.astype(F32)
    mid = rest.astype(BF16)
    lo = (rest - mid.astype(F32)).astype(BF16)
    return hi, mid, lo


def moved_columns(a, onehot):
    hi, mid, lo = split(a)
    return dot(hi, onehot) + dot(mid, onehot) + dot(lo, onehot)


def moved_transposed(a, onehot_t):
    hi, mid, lo = split(a)
    return dot(onehot_t, hi, NT) + dot(onehot_t, mid, NT) + dot(onehot_t, lo, NT)


def rotated_columns(a, cosine, sine):
    half = a.shape[1] // 2
    left, right = a[:, :half], a[:, half:]
    return jnp.concatenate([cosine * left - sine * right, sine * left + cosine * right], axis=1)


def angles(gram):
    half = gram.shape[0] // 2
    shape = (half, half)
    eye = lax.broadcasted_iota(jnp.int32, shape, 0) == lax.broadcasted_iota(jnp.int32, shape, 1)

    def diagonal(block):
        return jnp.sum(jnp.where(eye, block, 0.0), axis=0, keepdims=True)

    low = diagonal(gram[:half, :half])
    high = diagonal(gram[half:, half:])
    cross = diagonal(gram[:half, half:])
    spread = high - low
    sign = jnp.where(spread >= 0.0, 1.0, -1.0)
    root = jnp.sqrt(spread * spread + 4.0 * cross * cross)
    tangent = sign * 2.0 * cross / (jnp.abs(spread) + root)
    cosine = 1.0 / jnp.sqrt(1.0 + tangent * tangent)
    return cosine, tangent * cosine


def orders(partner):
    width = partner.shape[1]
    shape = (width, width)
    row = lax.broadcasted_iota(jnp.int32, shape, 0)
    col = lax.broadcasted_iota(jnp.int32, shape, 1)
    other = jnp.broadcast_to(partner, shape)
    swap = row == other
    one = jnp.ones(shape, BF16)

    def bits(mask):
        return jnp.where(mask, 1.0, 0.0).astype(BF16)

    swap_b = bits(swap)
    first_row = other > col
    rank_row = dot(bits(first_row), bits(row < col))
    mate_row = dot(rank_row.astype(BF16), swap_b)
    place_row = jnp.where(first_row, rank_row, mate_row + float(width // 2))
    first_col = dot(bits(swap & (col > row)), one) > 0.5
    rank_col = dot(bits(col < row), bits(first_col))
    mate_col = dot(swap_b, rank_col.astype(BF16))
    place_col = jnp.where(first_col, rank_col, mate_col + float(width // 2))
    forward = bits(place_col == col.astype(F32))
    backward = bits(place_row == row.astype(F32))
    return forward, backward


def diagonalizer(gram, step, moves, moves_t, rounds, want_rotation):
    rotation = None
    cosines, sines = [], []
    for r in range(rounds):
        move = moves[step, r]
        if r == 0:
            turned = moved_transposed(gram, moves_t[step, r])
            gram = moved_columns(turned, move)
        else:
            turned = moved_transposed(rotated_columns(gram, cosines[-1], sines[-1]), moves_t[step, r])
            gram = moved_columns(rotated_columns(turned, cosines[-1], sines[-1]), move)
        cosine, sine = angles(gram)
        cosines.append(cosine)
        sines.append(sine)
        if want_rotation:
            rotation = move.astype(F32) if r == 0 else moved_columns(rotation, move)
            rotation = rotated_columns(rotation, cosine, sine)
    if want_rotation:
        rotation = moved_columns(rotation, moves[step, rounds])
    return jnp.concatenate(cosines + sines, axis=0), rotation


def turn_rows(x, turns, step, moves, rounds):
    pairs, rows, width = x.shape
    half = width // 2
    for r in range(rounds):
        if r > 0:
            x = moved_columns(x, moves[step, r]).reshape(pairs, rows, width)
        cosine, sine = turns[:, r:r + 1, :], turns[:, rounds + r:rounds + r + 1, :]
        left, right = x[:, :, :half], x[:, :, half:]
        x = jnp.concatenate([cosine * left - sine * right, sine * left + cosine * right], axis=2)
        x = x.reshape(pairs * rows, width)
    return moved_columns(x, moves[step, rounds]).reshape(pairs, rows, width)


def kernel(sizes, x_ref, plan_ref, out_ref, stage, held, bottoms, landed, row_tops, row_low, row_landed, turns,
           moves, moves_t, grams, in_send, in_recv, mid_sem, gram_send, gram_recv, turn_send, turn_recv,
           row_send, row_recv):
    owners, groups, cols, rows_here, steps, rounds, width = sizes
    half = width // 2
    me = lax.axis_index("rows")
    col = lax.axis_index("cols")
    group, mine = me // owners, me % owners
    right = (col + 1) % cols

    def at(owner_shift, col_shift=0, group_shift=0):
        row = ((group + group_shift) % groups) * owners + (mine + owner_shift) % owners
        return row, (col + col_shift) % cols

    peers = {(o, 0, 0) for o in range(owners)} | {(0, c, 0) for c in (1, cols - 1)} | {(0, 0, g) for g in range(groups)}
    peers = sorted(peers - {(0, 0, 0)})
    barrier = pltpu.get_barrier_semaphore()
    for peer in peers:
        pl.semaphore_signal(barrier, inc=1, device_id=at(*peer), device_id_type=MESH)
    for k in range(owners):
        for h in range(2):
            stage[k, :, h * half:(h + 1) * half] = x_ref[pl.ds(2 * k + h, rows_here, stride=2 * owners), :]
    pl.semaphore_wait(barrier, len(peers))

    def rows_of(owner):
        return pl.ds(pl.multiple_of(owner * rows_here, rows_here), rows_here)

    incoming = []
    for d in range(1, owners):
        copy = pltpu.make_async_remote_copy(
            stage.at[(mine + d) % owners], held.at[rows_of(mine), :], in_send.at[d], in_recv.at[d],
            device_id=at(d), device_id_type=MESH)
        copy.start()
        incoming.append(copy)
    held[rows_of(mine), :] = stage[mine]

    for s in range(steps):
        before = None
        for r in range(rounds):
            forward, backward = orders(plan_ref[s, r:r + 1, :])
            if r == 0:
                moves[s, r] = forward
                moves_t[s, r] = backward
            else:
                moves[s, r] = dot(before[1], forward).astype(BF16)
                moves_t[s, r] = dot(backward, before[0]).astype(BF16)
            before = forward, backward
        moves[s, rounds] = before[1]

    for copy in incoming:
        copy.wait()

    x = held[...]
    chunks = 2 if owners % 2 == 0 else 1
    passing = []
    for s in range(steps):
        gram = exact_dot(x.T, x)
        if groups > 1:
            grams[s, group] = gram
            shared = []
            for g in range(1, groups):
                copy = pltpu.make_async_remote_copy(
                    grams.at[s, group], grams.at[s, group], gram_send.at[s, g], gram_recv.at[s, g],
                    device_id=at(0, 0, g), device_id_type=MESH)
                copy.start()
                shared.append(copy)
            for copy in shared:
                copy.wait()
            gram = grams[s, 0]
            for g in range(1, groups):
                gram = gram + grams[s, g]
        last = s + 1 == steps
        angle, rotation = diagonalizer(gram, s, moves, moves_t, rounds, not last)
        turns[s, mine] = angle
        told = []
        for d in range(1, owners):
            copy = pltpu.make_async_remote_copy(
                turns.at[s, mine], turns.at[s, mine], turn_send.at[s, d], turn_recv.at[s, d],
                device_id=at(d), device_id_type=MESH)
            copy.start()
            told.append(copy)
        if not last:
            bottoms[s] = exact_dot(x, rotation[:, half:])
            crossing = pltpu.make_async_remote_copy(
                bottoms.at[s], landed.at[s], mid_sem.at[s, 0], mid_sem.at[s, 1],
                device_id=(me, right), device_id_type=MESH)
            crossing.start()
            top = exact_dot(x, rotation[:, :half])
        if s > 0:
            for copy in passing:
                copy.wait()
        size = owners // chunks
        ordered = []
        for q in range(chunks):
            part = slice(q * size, (q + 1) * size)
            if s == 0:
                rows = stage[part]
            else:
                rows = jnp.concatenate([row_tops[s - 1, part], row_landed[s - 1, part]], axis=2)
            flat = moved_columns(rows.reshape(size * rows_here, width), moves[s, 0])
            ordered.append(flat.reshape(size, rows_here, width))
        for copy in told:
            copy.wait()
        passing = []
        for q in range(chunks):
            part = slice(q * size, (q + 1) * size)
            rows = turn_rows(ordered[q], turns[s, part], s, moves, rounds)
            row_low[s, part] = rows[:, :, half:]
            copy = pltpu.make_async_remote_copy(
                row_low.at[s, part], row_landed.at[s, part], row_send.at[s, q], row_recv.at[s, q],
                device_id=(me, right), device_id_type=MESH)
            copy.start()
            passing.append(copy)
            if last:
                for k in range(size):
                    out_ref[pl.ds(2 * (q * size + k), rows_here, stride=2 * owners), :] = rows[k, :, :half]
            else:
                row_tops[s, part] = rows[:, :, :half]
        if not last:
            crossing.wait()
            x = jnp.concatenate([top, landed[s]], axis=1)

    for q in range(chunks):
        passing[q].wait()
        for k in range(q * size, (q + 1) * size):
            out_ref[pl.ds(2 * k + 1, rows_here, stride=2 * owners), :] = row_landed[steps - 1, k]


def body(mesh_sizes, matrix, plan):
    rows_here, pair_here, halves, half = matrix.shape
    steps, rounds, width = plan.shape
    rows, cols = mesh_sizes
    owners, groups = pair_here, rows // pair_here
    assert rows % pair_here == 0 and halves == 2 and cols > 1
    sizes = (owners, groups, cols, rows_here, steps, rounds, width)
    dma = pltpu.SemaphoreType.DMA
    rows_all = owners * rows_here
    vmem = pl.BlockSpec(memory_space=pltpu.VMEM)
    out = pl.pallas_call(
        functools.partial(kernel, sizes),
        out_shape=jax.ShapeDtypeStruct((rows_here * pair_here * 2, half), F32),
        in_specs=[vmem, vmem],
        out_specs=vmem,
        scratch_shapes=[
            pltpu.VMEM((owners, rows_here, width), F32),
            pltpu.VMEM((rows_all, width), F32),
            pltpu.VMEM((steps - 1, rows_all, half), F32),
            pltpu.VMEM((steps - 1, rows_all, half), F32),
            pltpu.VMEM((steps, owners, rows_here, half), F32),
            pltpu.VMEM((steps, owners, rows_here, half), F32),
            pltpu.VMEM((steps, owners, rows_here, half), F32),
            pltpu.VMEM((steps, owners, 2 * rounds, half), F32),
            pltpu.VMEM((steps, rounds + 1, width, width), BF16),
            pltpu.VMEM((steps, rounds, width, width), BF16),
            pltpu.VMEM((steps, groups, width, width) if groups > 1 else (1, 1, 8, 128), F32),
            dma((owners,)), dma((owners,)), dma((steps, 2)), dma((steps, groups)), dma((steps, groups)),
            dma((steps, owners)), dma((steps, owners)), dma((steps, 2)), dma((steps, 2)),
        ],
        compiler_params=pltpu.CompilerParams(collective_id=0, has_side_effects=True, vmem_limit_bytes=48 << 20),
    )(matrix.reshape(rows_here * pair_here * 2, half), plan)
    return out.reshape(matrix.shape)


def solution(mesh):
    in_specs = (P("rows", "cols", None, None), P())
    out_specs = P("rows", "cols", None, None)
    sizes = (mesh.shape["rows"], mesh.shape["cols"])
    return jax.shard_map(functools.partial(body, sizes), mesh=mesh, in_specs=in_specs, out_specs=out_specs, check_vma=False)
```

profile of v0, /device:TPU:0, one launch (start us, length us, event | category | flops | bytes accessed | tf_op | source)
XLA Modules:
  0.0 44.3 jit_solution(1780508884633841777)
XLA Ops:
  0.0 0.0 copy-start
  0.0 1.0 %copy-done = f32[64,8,2,128]{3,2,1,0:T(2,128)S(1)} copy-done((f32[64,8,2,128]{3,2,1,0:T(2,128)S(1)}, f32[64,8,2,128]{3,2,1,0:T(2,128)}, u32[]{:S(2)}) %copy-start) | copy-done | bytes 524312
  1.0 0.0 copy-start.1
  1.0 0.7 %copy-done.1 = s32[2,4,256]{2,1,0:T(4,128)S(1)} copy-done((s32[2,4,256]{2,1,0:T(4,128)S(1)}, s32[2,4,256]{2,1,0:T(4,128)}, u32[]{:S(2)}) %copy-start.1) | copy-done | bytes 8216
  1.7 41.8 %shard_map.28 = f32[1024,128]{1,0:T(8,128)S(1)} custom-call(f32[1024,128]{1,0:T(8,128)S(1)} %bitcast.3, s32[2,4,256]{2,1,0:T(4,128)S(1)} %copy-done.1), custom_call_target="tpu_custom_call" | custom-call | tf_op jit(solution)/shard_map/pallas_call | solution.py:267
  43.5 0.8 %copy.4 = f32[64,8,2,128]{3,2,1,0:T(2,128)} copy(f32[64,8,2,128]{3,2,1,0:T(2,128)S(1)} %bitcast.2) | data formatting | bytes 1048576
Async XLA Ops:
  0.0 1.0 %copy-start = (f32[64,8,2,128]{3,2,1,0:T(2,128)S(1)}, f32[64,8,2,128]{3,2,1,0:T(2,128)}, u32[]{:S(2)}) copy-start(f32[64,8,2,128]{3,2,1,0:T(2,128)} %param.2) | copy-start | bytes 1572868
  1.0 0.7 %copy-start.1 = (s32[2,4,256]{2,1,0:T(4,128)S(1)}, s32[2,4,256]{2,1,0:T(4,128)}, u32[]{:S(2)}) copy-start(s32[2,4,256]{2,1,0:T(4,128)} %plan_ref.1) | copy-start | bytes 24580
where the time goes:
time: 44.5 us; the launch traced here: 44.3 us
  Pallas kernels  41.8 us (94%)
  local copies, waits for them, and re-layouts  2.53 us (6%)
    pallas_call x1, Pallas kernels, body(): pl.pallas_call(functools.partial(kernel, sizes), out_shape=jax.ShapeDtype...  41.8 us
    unnamed x5, local copies, waits for them, and re-layouts  2.53 us

commit v1 on v0

v1 whole, which is shorter than its diff:
```python
import functools

import jax
import jax.numpy as jnp
from jax import lax
from jax.experimental import pallas as pl
from jax.experimental.pallas import tpu as pltpu
from jax.sharding import PartitionSpec as P

MESH = pl.DeviceIdType.MESH
NN = (((1,), (0,)), ((), ()))
NT = (((1,), (1,)), ((), ()))
F32 = jnp.float32
BF16 = jnp.bfloat16


def dot(a, b, dims=NN, precision=None):
    return lax.dot_general(a, b, dims, precision=precision, preferred_element_type=F32)


def exact_dot(a, b, dims=NN):
    return dot(a, b, dims, lax.Precision.HIGHEST)


def moved_columns(a, onehot):
    hi = a.astype(BF16)
    rest = a - hi.astype(F32)
    mid = rest.astype(BF16)
    lo = (rest - mid.astype(F32)).astype(BF16)
    return dot(hi, onehot) + dot(mid, onehot) + dot(lo, onehot)


def moved_columns_short(a, onehot):
    hi = a.astype(BF16)
    mid = (a - hi.astype(F32)).astype(BF16)
    return dot(hi, onehot) + dot(mid, onehot)


def gathered_columns(a, source):
    rows, width = a.shape
    half = width // 2
    parts = []
    for h in range(2):
        index = source[:, h * half:(h + 1) * half]
        lane = jnp.broadcast_to(index % half, (rows, half))
        second = jnp.broadcast_to(index >= half, (rows, half))
        left, right = (
            jnp.take_along_axis(a[:, k * half:(k + 1) * half], lane, axis=1, mode="promise_in_bounds") for k in range(2))
        parts.append(jnp.where(second, right, left))
    return jnp.concatenate(parts, axis=1)


def rotated_columns(a, cosine, sine):
    half = a.shape[-1] // 2
    left, right = a[..., :half], a[..., half:]
    return jnp.concatenate([cosine * left - sine * right, sine * left + cosine * right], axis=-1)


def folded(a):
    return jnp.sum(a.reshape(-1, 8, a.shape[-1]), axis=0)


def products(factors):
    low = high = cross = 0.0
    for a, b in factors:
        half = a.shape[1] // 2
        low = low + folded(a[:, :half] * b[:, :half])
        high = high + folded(a[:, half:] * b[:, half:])
        cross = cross + folded(a[:, :half] * b[:, half:])
    return low, high, cross


def angles(sums):
    low, high, cross = (jnp.sum(v, axis=0, keepdims=True) for v in sums)
    spread = high - low
    sign = jnp.where(spread >= 0.0, 1.0, -1.0)
    root = jnp.sqrt(spread * spread + 4.0 * cross * cross)
    tangent = sign * 2.0 * cross / (jnp.abs(spread) + root)
    cosine = 1.0 / jnp.sqrt(1.0 + tangent * tangent)
    return cosine, tangent * cosine


def orders(partner):
    width = partner.shape[1]
    shape = (width, width)
    row = lax.broadcasted_iota(jnp.int32, shape, 0)
    col = lax.broadcasted_iota(jnp.int32, shape, 1)
    other = jnp.broadcast_to(partner, shape)
    swap = row == other
    one = jnp.ones(shape, BF16)

    def bits(mask):
        return jnp.where(mask, 1.0, 0.0).astype(BF16)

    swap_b = bits(swap)
    first_row = other > col
    rank_row = dot(bits(first_row), bits(row < col))
    mate_row = dot(rank_row.astype(BF16), swap_b)
    place_row = jnp.where(first_row, rank_row, mate_row + float(width // 2))
    first_col = dot(bits(swap & (col > row)), one) > 0.5
    rank_col = dot(bits(col < row), bits(first_col))
    mate_col = dot(swap_b, rank_col.astype(BF16))
    place_col = jnp.where(first_col, rank_col, mate_col + float(width // 2))
    forward = bits(place_col == col.astype(F32))
    backward = bits(place_row == row.astype(F32))
    return forward, backward


def kernel(sizes, x_hbm, plan_hbm, out_ref, x_ref, plan_ref, stage, held, state, bottoms, landed, tops, row_state,
           row_tops, row_low, row_landed, turns, moves, sources, grams, load_sem, in_send, in_recv, mid_send, mid_recv,
           gram_send, gram_recv, turn_send, turn_recv, row_send, row_recv):
    owners, groups, cols, rows_here, steps, rounds, width = sizes
    half = width // 2
    rows_all = owners * rows_here
    me = lax.axis_index("rows")
    col = lax.axis_index("cols")
    group, mine = me // owners, me % owners
    right = (col + 1) % cols

    def at(owner_shift, col_shift=0, group_shift=0):
        row = ((group + group_shift) % groups) * owners + (mine + owner_shift) % owners
        return row, (col + col_shift) % cols

    peers = {(o, 0, 0) for o in range(owners)} | {(0, c, 0) for c in (1, cols - 1)} | {(0, 0, g) for g in range(groups)}
    peers = sorted(peers - {(0, 0, 0)})
    barrier = pltpu.get_barrier_semaphore()
    for peer in peers:
        pl.semaphore_signal(barrier, inc=1, device_id=at(*peer), device_id_type=MESH)
    load = pltpu.make_async_copy(x_hbm, x_ref, load_sem.at[0])
    load.start()
    load_plan = pltpu.make_async_copy(plan_hbm, plan_ref, load_sem.at[1])
    load_plan.start()
    load.wait()
    for k in range(owners):
        for h in range(2):
            stage[k, :, h * half:(h + 1) * half] = x_ref[pl.ds(2 * k + h, rows_here, stride=2 * owners), :]
    with jax.named_scope("barrier_wait"):
        pl.semaphore_wait(barrier, len(peers))

    def rows_of(owner):
        return pl.ds(pl.multiple_of(owner * rows_here, rows_here), rows_here)

    incoming = []
    for d in range(1, owners):
        copy = pltpu.make_async_remote_copy(
            stage.at[(mine + d) % owners], held.at[rows_of(mine), :], in_send.at[d], in_recv.at[d],
            device_id=at(d), device_id_type=MESH)
        copy.start()
        incoming.append(copy)

    load_plan.wait()
    with jax.named_scope("orders"):
        ladder = lax.broadcasted_iota(jnp.int32, (8, width), 1).astype(F32).astype(BF16)
        for s in range(steps):
            before = None
            for r in range(rounds + 1):
                if r < rounds:
                    forward, backward = orders(plan_ref[s, r:r + 1, :])
                    move = forward if r == 0 else dot(before, forward).astype(BF16)
                    before = backward
                else:
                    move = before
                moves[s, r] = move
                sources[s, r] = dot(ladder, move).astype(jnp.int32)

    def advanced(ref, turn, s, r):
        parts = []
        cut = ref.shape[0] // 2
        for h in range(2):
            part = ref[h * cut:(h + 1) * cut, :]
            if turn is not None:
                part = rotated_columns(part, *turn)
            if h == 0:
                parts.append(moved_columns(part, moves[s, r]))
            else:
                parts.append(gathered_columns(part, sources[s, r, 0:1, :]))
        return parts

    def kept(ref, parts):
        cut = ref.shape[0] // 2
        for h in range(2):
            ref[h * cut:(h + 1) * cut, :] = parts[h]

    def tell(s, r, turn):
        cosine, sine = turn
        turns[s, r, mine] = jnp.concatenate([cosine, sine], axis=0)
        told = []
        for d in range(1, owners):
            copy = pltpu.make_async_remote_copy(
                turns.at[s, r, mine], turns.at[s, r, mine], turn_send.at[s, r, d], turn_recv.at[s, r, d],
                device_id=at(d), device_id_type=MESH)
            copy.start()
            told.append(copy)
        return told

    def solved(s, sums):
        if sums is None:
            x = tops[...]
            gram = exact_dot(x.T, x)
            grams[s, group] = gram
            shared = []
            for g in range(1, groups):
                copy = pltpu.make_async_remote_copy(
                    grams.at[s, group], grams.at[s, group], gram_send.at[s, g], gram_recv.at[s, g],
                    device_id=at(0, 0, g), device_id_type=MESH)
                copy.start()
                shared.append(copy)
            for copy in shared:
                copy.wait()
            gram = grams[s, 0]
            for g in range(1, groups):
                gram = gram + grams[s, g]
            state[0:width, :] = gram
            shape = (width, width)
            eye = lax.broadcasted_iota(jnp.int32, shape, 0) == lax.broadcasted_iota(jnp.int32, shape, 1)
            state[width:2 * width, :] = jnp.where(eye, 1.0, 0.0)
        turn, all_turns, told = None, [], []
        for r in range(rounds):
            if r > 0 or sums is None:
                parts = advanced(state, turn, s, r)
                kept(state, parts)
                factors = [tuple(parts)] if groups > 1 else [(part, part) for part in parts]
                sums = products(factors)
            turn = angles(sums)
            told.append(tell(s, r, turn))
            all_turns.append(turn)
        return all_turns, told

    def final_parts(s, all_turns):
        if groups > 1:
            turn = None
            for r in range(rounds):
                kept(tops, advanced(tops, turn, s, r))
                turn = all_turns[r]
            return advanced(tops, turn, s, rounds)
        return advanced(state, all_turns[-1], s, rounds)

    chunks = 2 if owners % 2 == 0 else 1
    size = owners // chunks

    def short_moved(rows, s, r):
        return moved_columns_short(rows.reshape(size * rows_here, width), moves[s, r]).reshape(size, rows_here, width)

    with jax.named_scope("rows_first"):
        for q in range(chunks):
            part = slice(q * size, (q + 1) * size)
            row_state[part] = short_moved(stage[part], 0, 0)

    def first_step(rows):
        if groups > 1:
            tops[rows, :] = held[rows, :]
            return None
        moved = moved_columns(held[rows, :], moves[0, 0])
        state[rows, :] = moved
        return products([(moved, moved)])

    with jax.named_scope("a2a_wait"):
        held[rows_of(mine), :] = stage[mine]
        sums = first_step(rows_of(mine))
        for d in range(1, owners):
            incoming[d - 1].wait_recv()
            more = first_step(rows_of((mine + owners - d) % owners))
            if more is not None:
                sums = tuple(a + b for a, b in zip(sums, more))

    passing = []
    for s in range(steps):
        last = s + 1 == steps
        with jax.named_scope(f"solve{s}"):
            all_turns, told = solved(s, sums)
        if not last:
            with jax.named_scope(f"cross_send{s}"):
                parts = final_parts(s, all_turns)
                cut = rows_all // 2
                crossing = []
                for h in range(2):
                    bottoms[s, h] = parts[h][:, half:]
                    copy = pltpu.make_async_remote_copy(
                        bottoms.at[s, h], landed.at[s, h], mid_send.at[s, h], mid_recv.at[s, h],
                        device_id=(me, right), device_id_type=MESH)
                    copy.start()
                    crossing.append(copy)
                    tops[h * cut:(h + 1) * cut, :half] = parts[h][:, :half]
        if s > 0:
            with jax.named_scope(f"pass_wait{s}"):
                for copy in passing:
                    copy.wait()
            for q in range(chunks):
                part = slice(q * size, (q + 1) * size)
                rows = jnp.concatenate([row_tops[s - 1, part], row_landed[s - 1, part]], axis=2)
                row_state[part] = short_moved(rows, s, 0)
        passing = []
        for r in range(rounds):
            with jax.named_scope(f"told{s}_{r}"):
                for copy in told[r]:
                    copy.wait()
            with jax.named_scope(f"turn{s}_{r}"):
              for q in range(chunks):
                part = slice(q * size, (q + 1) * size)
                rows = rotated_columns(row_state[part], turns[s, r, part, 0:1, :], turns[s, r, part, 1:2, :])
                rows = short_moved(rows, s, r + 1)
                if r + 1 < rounds:
                    row_state[part] = rows
                    continue
                row_low[s, part] = rows[:, :, half:]
                copy = pltpu.make_async_remote_copy(
                    row_low.at[s, part], row_landed.at[s, part], row_send.at[s, q], row_recv.at[s, q],
                    device_id=(me, right), device_id_type=MESH)
                copy.start()
                passing.append(copy)
                if last:
                    for k in range(size):
                        out_ref[pl.ds(2 * (q * size + k), rows_here, stride=2 * owners), :] = rows[k, :, :half]
                else:
                    row_tops[s, part] = rows[:, :, :half]
        if not last:
            sums = None
            with jax.named_scope(f"cross_wait{s}"):
                for copy in crossing:
                    copy.wait()
            with jax.named_scope(f"cross_join{s}"):
                for h in range(2):
                    tops[h * cut:(h + 1) * cut, half:] = landed[s, h]
                if groups == 1:
                    parts = advanced(tops, None, s + 1, 0)
                    kept(state, parts)
                    sums = products([(part, part) for part in parts])

    for copy in incoming:
        copy.wait_send()
    for q in range(chunks):
        with jax.named_scope("last_pass"):
            passing[q].wait()
        for k in range(q * size, (q + 1) * size):
            out_ref[pl.ds(2 * k + 1, rows_here, stride=2 * owners), :] = row_landed[steps - 1, k]


def body(mesh_sizes, matrix, plan):
    rows_here, pair_here, halves, half = matrix.shape
    steps, rounds, width = plan.shape
    rows, cols = mesh_sizes
    owners, groups = pair_here, rows // pair_here
    assert rows % pair_here == 0 and halves == 2 and cols > 1
    sizes = (owners, groups, cols, rows_here, steps, rounds, width)
    dma = pltpu.SemaphoreType.DMA
    rows_all = owners * rows_here
    assert groups == 1 or rows_all >= 2 * width
    flat = (rows_here * pair_here * 2, half)
    anywhere = pl.BlockSpec(memory_space=pltpu.HBM)
    out = pl.pallas_call(
        functools.partial(kernel, sizes),
        out_shape=jax.ShapeDtypeStruct(flat, F32),
        in_specs=[anywhere, anywhere],
        out_specs=pl.BlockSpec(memory_space=pltpu.VMEM),
        scratch_shapes=[
            pltpu.VMEM(flat, F32),
            pltpu.VMEM((steps, rounds, width), jnp.int32),
            pltpu.VMEM((owners, rows_here, width), F32),
            pltpu.VMEM((rows_all, width), F32),
            pltpu.VMEM((rows_all if groups == 1 else 2 * width, width), F32),
            pltpu.VMEM((steps - 1, 2, rows_all // 2, half), F32),
            pltpu.VMEM((steps - 1, 2, rows_all // 2, half), F32),
            pltpu.VMEM((rows_all, width), F32),
            pltpu.VMEM((owners, rows_here, width), F32),
            pltpu.VMEM((steps - 1, owners, rows_here, half), F32),
            pltpu.VMEM((steps, owners, rows_here, half), F32),
            pltpu.VMEM((steps, owners, rows_here, half), F32),
            pltpu.VMEM((steps, rounds, owners, 2, half), F32),
            pltpu.VMEM((steps, rounds + 1, width, width), BF16),
            pltpu.VMEM((steps, rounds + 1, 8, width), jnp.int32),
            pltpu.VMEM((steps, groups, width, width) if groups > 1 else (1, 1, 8, 128), F32),
            dma((2,)), dma((owners,)), dma((owners,)), dma((steps, 2)), dma((steps, 2)),
            dma((steps, groups)), dma((steps, groups)),
            dma((steps, rounds, owners)), dma((steps, rounds, owners)), dma((steps, 2)), dma((steps, 2)),
        ],
        compiler_params=pltpu.CompilerParams(collective_id=0, has_side_effects=True, vmem_limit_bytes=40 << 20),
    )(matrix.reshape(flat), plan)
    return out.reshape(matrix.shape)


def solution(mesh):
    in_specs = (P("rows", "cols", None, None), P())
    out_specs = P("rows", "cols", None, None)
    sizes = (mesh.shape["rows"], mesh.shape["cols"])
    return jax.shard_map(functools.partial(body, sizes), mesh=mesh, in_specs=in_specs, out_specs=out_specs, check_vma=False)
```

time: 44.5 us -> 38.2 us (0.86)
  Pallas kernels: 41.8 us -> 35.4 us
    pallas_call x1, Pallas kernels: 41.8 us -> 35.4 us  [body(): pl.pallas_call(functools.partial(kernel, sizes), out_shape=jax.ShapeDtype...]
where the time goes in v1:
time: 38.2 us; the launch traced here: 38 us
  Pallas kernels  35.4 us (93%)
  local copies, waits for them, and re-layouts  2.53 us (7%)
    pallas_call x1, Pallas kernels, body(): pl.pallas_call(functools.partial(kernel, sizes), out_shape=jax.ShapeDtype...  35.4 us
    unnamed x5, local copies, waits for them, and re-layouts  2.53 us

profile of v1, /device:TPU:0, one launch (start us, length us, event | category | flops | bytes accessed | tf_op | source)
XLA Modules:
  0.0 38.0 jit_solution(17159847078464867755)
XLA Ops:
  0.0 0.0 copy-start
  0.0 1.0 %copy-done = f32[64,8,2,128]{3,2,1,0:T(2,128)S(1)} copy-done((f32[64,8,2,128]{3,2,1,0:T(2,128)S(1)}, f32[64,8,2,128]{3,2,1,0:T(2,128)}, u32[]{:S(2)}) %copy-start) | copy-done | bytes 524312
  1.0 0.0 copy-start.1
  1.0 0.7 %copy-done.1 = s32[2,4,256]{2,1,0:T(4,128)S(1)} copy-done((s32[2,4,256]{2,1,0:T(4,128)S(1)}, s32[2,4,256]{2,1,0:T(4,128)}, u32[]{:S(2)}) %copy-start.1) | copy-done | bytes 8216
  1.7 35.4 %shard_map.28 = f32[1024,128]{1,0:T(8,128)S(1)} custom-call(f32[1024,128]{1,0:T(8,128)S(1)} %bitcast.3, s32[2,4,256]{2,1,0:T(4,128)S(1)} %copy-done.1), custom_call_target="tpu_custom_call" | custom-call | tf_op jit(solution)/shard_map/pallas_call | solution.py:350
  37.2 0.8 %copy.4 = f32[64,8,2,128]{3,2,1,0:T(2,128)} copy(f32[64,8,2,128]{3,2,1,0:T(2,128)S(1)} %bitcast.2) | data formatting | bytes 1048576
Async XLA Ops:
  0.0 1.0 %copy-start = (f32[64,8,2,128]{3,2,1,0:T(2,128)S(1)}, f32[64,8,2,128]{3,2,1,0:T(2,128)}, u32[]{:S(2)}) copy-start(f32[64,8,2,128]{3,2,1,0:T(2,128)} %param.2) | copy-start | bytes 1572868
  1.0 0.7 %copy-start.1 = (s32[2,4,256]{2,1,0:T(4,128)S(1)}, s32[2,4,256]{2,1,0:T(4,128)}, u32[]{:S(2)}) copy-start(s32[2,4,256]{2,1,0:T(4,128)} %plan_hbm.1) | copy-start | bytes 24580

commit v2 on v1

--- a/solution.py
+++ b/solution.py
@@ -143,7 +143,7 @@
     incoming = []
     for d in range(1, owners):
         copy = pltpu.make_async_remote_copy(
-            stage.at[(mine + d) % owners], held.at[rows_of(mine), :], in_send.at[d], in_recv.at[d],
+            stage.at[(mine + d) % owners], held.at[rows_of(mine), :], in_send.at[0], in_recv.at[d],
             device_id=at(d), device_id_type=MESH)
         copy.start()
         incoming.append(copy)
@@ -184,14 +184,20 @@
     def tell(s, r, turn):
         cosine, sine = turn
         turns[s, r, mine] = jnp.concatenate([cosine, sine], axis=0)
-        told = []
         for d in range(1, owners):
-            copy = pltpu.make_async_remote_copy(
-                turns.at[s, r, mine], turns.at[s, r, mine], turn_send.at[s, r, d], turn_recv.at[s, r, d],
-                device_id=at(d), device_id_type=MESH)
-            copy.start()
-            told.append(copy)
-        return told
+            pltpu.make_async_remote_copy(
+                turns.at[s, r, mine], turns.at[s, r, mine], turn_send.at[s], turn_recv.at[s, r],
+                device_id=at(d), device_id_type=MESH).start()
+
+    def all_told(s, r):
+        block = turns.at[s, r, 0:owners - 1]
+        return pltpu.make_async_remote_copy(
+            block, block, turn_send.at[s], turn_recv.at[s, r], device_id=at(1), device_id_type=MESH)
+
+    def all_tells(s):
+        block = turns.at[s, :, 0:owners - 1]
+        return pltpu.make_async_remote_copy(
+            block, block, turn_send.at[s], turn_recv.at[s, 0], device_id=at(1), device_id_type=MESH)
 
     def solved(s, sums):
         if sums is None:
@@ -214,7 +220,7 @@
             shape = (width, width)
             eye = lax.broadcasted_iota(jnp.int32, shape, 0) == lax.broadcasted_iota(jnp.int32, shape, 1)
             state[width:2 * width, :] = jnp.where(eye, 1.0, 0.0)
-        turn, all_turns, told = None, [], []
+        turn, all_turns = None, []
         for r in range(rounds):
             if r > 0 or sums is None:
                 parts = advanced(state, turn, s, r)
@@ -222,9 +228,9 @@
                 factors = [tuple(parts)] if groups > 1 else [(part, part) for part in parts]
                 sums = products(factors)
             turn = angles(sums)
-            told.append(tell(s, r, turn))
+            tell(s, r, turn)
             all_turns.append(turn)
-        return all_turns, told
+        return all_turns
 
     def final_parts(s, all_turns):
         if groups > 1:
@@ -238,13 +244,18 @@
     chunks = 2 if owners % 2 == 0 else 1
     size = owners // chunks
 
-    def short_moved(rows, s, r):
-        return moved_columns_short(rows.reshape(size * rows_here, width), moves[s, r]).reshape(size, rows_here, width)
+    def short_moved(q, rows, s, r):
+        flat = rows.reshape(size * rows_here, width)
+        if q % 2 == 0:
+            flat = moved_columns_short(flat, moves[s, r])
+        else:
+            flat = gathered_columns(flat, sources[s, r, 0:1, :])
+        return flat.reshape(size, rows_here, width)
 
     with jax.named_scope("rows_first"):
         for q in range(chunks):
             part = slice(q * size, (q + 1) * size)
-            row_state[part] = short_moved(stage[part], 0, 0)
+            row_state[part] = short_moved(q, stage[part], 0, 0)
 
     def first_step(rows):
         if groups > 1:
@@ -267,7 +278,7 @@
     for s in range(steps):
         last = s + 1 == steps
         with jax.named_scope(f"solve{s}"):
-            all_turns, told = solved(s, sums)
+            all_turns = solved(s, sums)
         if not last:
             with jax.named_scope(f"cross_send{s}"):
                 parts = final_parts(s, all_turns)
@@ -288,31 +299,34 @@
             for q in range(chunks):
                 part = slice(q * size, (q + 1) * size)
                 rows = jnp.concatenate([row_tops[s - 1, part], row_landed[s - 1, part]], axis=2)
-                row_state[part] = short_moved(rows, s, 0)
+                row_state[part] = short_moved(q, rows, s, 0)
         passing = []
         for r in range(rounds):
             with jax.named_scope(f"told{s}_{r}"):
-                for copy in told[r]:
-                    copy.wait()
+                all_told(s, r).wait_recv()
             with jax.named_scope(f"turn{s}_{r}"):
-              for q in range(chunks):
-                part = slice(q * size, (q + 1) * size)
-                rows = rotated_columns(row_state[part], turns[s, r, part, 0:1, :], turns[s, r, part, 1:2, :])
-                rows = short_moved(rows, s, r + 1)
-                if r + 1 < rounds:
-                    row_state[part] = rows
-                    continue
-                row_low[s, part] = rows[:, :, half:]
-                copy = pltpu.make_async_remote_copy(
-                    row_low.at[s, part], row_landed.at[s, part], row_send.at[s, q], row_recv.at[s, q],
-                    device_id=(me, right), device_id_type=MESH)
-                copy.start()
-                passing.append(copy)
-                if last:
-                    for k in range(size):
-                        out_ref[pl.ds(2 * (q * size + k), rows_here, stride=2 * owners), :] = rows[k, :, :half]
-                else:
-                    row_tops[s, part] = rows[:, :, :half]
+                turned = []
+                for q in range(chunks):
+                    part = slice(q * size, (q + 1) * size)
+                    rows = rotated_columns(row_state[part], turns[s, r, part, 0:1, :], turns[s, r, part, 1:2, :])
+                    turned.append(short_moved(q, rows, s, r + 1))
+                for q in range(chunks):
+                    part = slice(q * size, (q + 1) * size)
+                    if r + 1 < rounds:
+                        row_state[part] = turned[q]
+                        continue
+                    row_low[s, part] = turned[q][:, :, half:]
+                    copy = pltpu.make_async_remote_copy(
+                        row_low.at[s, part], row_landed.at[s, part], row_send.at[s, q], row_recv.at[s, q],
+                        device_id=(me, right), device_id_type=MESH)
+                    copy.start()
+                    passing.append(copy)
+                    if last:
+                        for k in range(size):
+                            at_rows = pl.ds(2 * (q * size + k), rows_here, stride=2 * owners)
+                            out_ref[at_rows, :] = turned[q][k, :, :half]
+                    else:
+                        row_tops[s, part] = turned[q][:, :, :half]
         if not last:
             sums = None
             with jax.named_scope(f"cross_wait{s}"):
@@ -326,8 +340,10 @@
                     kept(state, parts)
                     sums = products([(part, part) for part in parts])
 
-    for copy in incoming:
-        copy.wait_send()
+    for s in range(steps):
+        all_tells(s).wait_send()
+    sent = stage.at[0:owners - 1]
+    pltpu.make_async_remote_copy(sent, sent, in_send.at[0], in_recv.at[0], device_id=at(1), device_id_type=MESH).wait_send()
     for q in range(chunks):
         with jax.named_scope("last_pass"):
             passing[q].wait()
@@ -369,12 +385,13 @@
             pltpu.VMEM((steps, rounds + 1, width, width), BF16),
             pltpu.VMEM((steps, rounds + 1, 8, width), jnp.int32),
             pltpu.VMEM((steps, groups, width, width) if groups > 1 else (1, 1, 8, 128), F32),
-            dma((2,)), dma((owners,)), dma((owners,)), dma((steps, 2)), dma((steps, 2)),
-            dma((steps, groups)), dma((steps, groups)),
-            dma((steps, rounds, owners)), dma((steps, rounds, owners)), dma((steps, 2)), dma((steps, 2)),
+            dma((2,)), dma((1,)), dma((owners,)), dma((steps - 1, 2)), dma((steps - 1, 2)),
+            dma((steps, groups) if groups > 1 else (1, 1)), dma((steps, groups) if groups > 1 else (1, 1)),
+            dma((steps,)), dma((steps, rounds)), dma((steps, 2)), dma((steps, 2)),
         ],
         compiler_params=pltpu.CompilerParams(collective_id=0, has_side_effects=True, vmem_limit_bytes=40 << 20),
-    )(matrix.reshape(flat), plan)
+    )(pltpu.with_memory_space_constraint(matrix.reshape(flat), pltpu.HBM),
+      pltpu.with_memory_space_constraint(plan, pltpu.HBM))
     return out.reshape(matrix.shape)
 
 

time: 38.2 us -> 35 us (0.916)
  local copies, waits for them, and re-layouts: 2.53 us -> 0.8 us
  Pallas kernels: 35.4 us -> 34 us
    unnamed x5 -> x1, local copies, waits for them, and re-layouts: 2.53 us -> 0.8 us
    pallas_call x1, Pallas kernels: 35.4 us -> 34 us  [body(): pl.pallas_call(functools.partial(kernel, sizes), out_shape=jax.ShapeDtype...]
where the time goes in v2:
time: 35 us; the launch traced here: 34.8 us
  Pallas kernels  34 us (97%)
  local copies, waits for them, and re-layouts  0.8 us (2%)
    pallas_call x1, Pallas kernels, body(): pl.pallas_call(functools.partial(kernel, sizes), out_shape=jax.ShapeDtype...  34 us
    unnamed x1, local copies, waits for them, and re-layouts  0.8 us

profile of v2, /device:TPU:0, one launch (start us, length us, event | category | flops | bytes accessed | tf_op | source)
XLA Modules:
  0.0 34.8 jit_solution(14605149822501295492)
XLA Ops:
  0.0 34.0 %shard_map.28 = f32[1024,128]{1,0:T(8,128)S(1)} custom-call(f32[1024,128]{1,0:T(8,128)} %bitcast.3, s32[2,4,256]{2,1,0:T(4,128)} %plan_hbm.1), custom_call_target="tpu_custom_call" | custom-call | tf_op jit(solution)/shard_map/pallas_call | solution.py:366
  34.0 0.8 %copy.4 = f32[64,8,2,128]{3,2,1,0:T(2,128)} copy(f32[64,8,2,128]{3,2,1,0:T(2,128)S(1)} %bitcast.2) | data formatting | bytes 1048576

commit v3 on v2

--- a/solution.py
+++ b/solution.py
@@ -76,7 +76,7 @@
     sign = jnp.where(spread >= 0.0, 1.0, -1.0)
     root = jnp.sqrt(spread * spread + 4.0 * cross * cross)
     tangent = sign * 2.0 * cross / (jnp.abs(spread) + root)
-    cosine = 1.0 / jnp.sqrt(1.0 + tangent * tangent)
+    cosine = lax.rsqrt(1.0 + tangent * tangent)
     return cosine, tangent * cosine
 
 
@@ -107,8 +107,8 @@
 
 
 def kernel(sizes, x_hbm, plan_hbm, out_ref, x_ref, plan_ref, stage, held, state, bottoms, landed, tops, row_state,
-           row_tops, row_low, row_landed, turns, moves, sources, grams, load_sem, in_send, in_recv, mid_send, mid_recv,
-           gram_send, gram_recv, turn_send, turn_recv, row_send, row_recv):
+           row_tops, row_low, row_landed, finals, turns, moves, sources, grams, load_sem, in_send, in_recv, mid_send, mid_recv,
+           gram_send, gram_recv, turn_send, turn_recv, row_send, row_recv, direct):
     owners, groups, cols, rows_here, steps, rounds, width = sizes
     half = width // 2
     rows_all = owners * rows_here
@@ -241,8 +241,9 @@
             return advanced(tops, turn, s, rounds)
         return advanced(state, all_turns[-1], s, rounds)
 
-    chunks = 2 if owners % 2 == 0 else 1
+    chunks = 2
     size = owners // chunks
+    side = mine // size
 
     def short_moved(q, rows, s, r):
         flat = rows.reshape(size * rows_here, width)
@@ -292,6 +293,17 @@
                     copy.start()
                     crossing.append(copy)
                     tops[h * cut:(h + 1) * cut, :half] = parts[h][:, :half]
+        else:
+            with jax.named_scope("direct_send"):
+                parts = final_parts(s, all_turns)
+                cut = rows_all // 2
+                for h in range(2):
+                    finals[h * cut:(h + 1) * cut, :] = parts[h][:, half:]
+                for j in range(size):
+                    owner = side * size + (mine + j) % size
+                    pltpu.make_async_remote_copy(
+                        finals.at[rows_of(owner), :], row_landed.at[s, mine], direct.at[0], direct.at[1],
+                        device_id=(group * owners + owner, right), device_id_type=MESH).start()
         if s > 0:
             with jax.named_scope(f"pass_wait{s}"):
                 for copy in passing:
@@ -316,10 +328,14 @@
                         row_state[part] = turned[q]
                         continue
                     row_low[s, part] = turned[q][:, :, half:]
+                    slot = 0 if last else q
                     copy = pltpu.make_async_remote_copy(
-                        row_low.at[s, part], row_landed.at[s, part], row_send.at[s, q], row_recv.at[s, q],
+                        row_low.at[s, part], row_landed.at[s, part], row_send.at[s, slot], row_recv.at[s, slot],
                         device_id=(me, right), device_id_type=MESH)
-                    copy.start()
+                    if last:
+                        pl.when(side != q)(copy.start)
+                    else:
+                        copy.start()
                     passing.append(copy)
                     if last:
                         for k in range(size):
@@ -344,11 +360,20 @@
         all_tells(s).wait_send()
     sent = stage.at[0:owners - 1]
     pltpu.make_async_remote_copy(sent, sent, in_send.at[0], in_recv.at[0], device_id=at(1), device_id_type=MESH).wait_send()
-    for q in range(chunks):
-        with jax.named_scope("last_pass"):
-            passing[q].wait()
+    def put_bottoms(q):
         for k in range(q * size, (q + 1) * size):
             out_ref[pl.ds(2 * k + 1, rows_here, stride=2 * owners), :] = row_landed[steps - 1, k]
+
+    near = row_landed.at[steps - 1, 0:size]
+    with jax.named_scope("direct_wait"):
+        pltpu.make_async_remote_copy(
+            near, near, direct.at[0], direct.at[1], device_id=(me, right), device_id_type=MESH).wait()
+    for q in range(chunks):
+        pl.when(side == q)(functools.partial(put_bottoms, q))
+    with jax.named_scope("last_pass"):
+        passing[0].wait()
+    for q in range(chunks):
+        pl.when(side != q)(functools.partial(put_bottoms, q))
 
 
 def body(mesh_sizes, matrix, plan):
@@ -356,7 +381,7 @@
     steps, rounds, width = plan.shape
     rows, cols = mesh_sizes
     owners, groups = pair_here, rows // pair_here
-    assert rows % pair_here == 0 and halves == 2 and cols > 1
+    assert rows % pair_here == 0 and pair_here % 2 == 0 and halves == 2 and cols > 1
     sizes = (owners, groups, cols, rows_here, steps, rounds, width)
     dma = pltpu.SemaphoreType.DMA
     rows_all = owners * rows_here
@@ -381,13 +406,14 @@
             pltpu.VMEM((steps - 1, owners, rows_here, half), F32),
             pltpu.VMEM((steps, owners, rows_here, half), F32),
             pltpu.VMEM((steps, owners, rows_here, half), F32),
+            pltpu.VMEM((rows_all, half), F32),
             pltpu.VMEM((steps, rounds, owners, 2, half), F32),
             pltpu.VMEM((steps, rounds + 1, width, width), BF16),
             pltpu.VMEM((steps, rounds + 1, 8, width), jnp.int32),
             pltpu.VMEM((steps, groups, width, width) if groups > 1 else (1, 1, 8, 128), F32),
             dma((2,)), dma((1,)), dma((owners,)), dma((steps - 1, 2)), dma((steps - 1, 2)),
             dma((steps, groups) if groups > 1 else (1, 1)), dma((steps, groups) if groups > 1 else (1, 1)),
-            dma((steps,)), dma((steps, rounds)), dma((steps, 2)), dma((steps, 2)),
+            dma((steps,)), dma((steps, rounds)), dma((steps, 2)), dma((steps, 2)), dma((2,)),
         ],
         compiler_params=pltpu.CompilerParams(collective_id=0, has_side_effects=True, vmem_limit_bytes=40 << 20),
     )(pltpu.with_memory_space_constraint(matrix.reshape(flat), pltpu.HBM),

time: 35 us -> 33.8 us (0.966)
  Pallas kernels: 34 us -> 32.8 us
    pallas_call x1, Pallas kernels: 34 us -> 32.8 us  [body(): pl.pallas_call(functools.partial(kernel, sizes), out_shape=jax.ShapeDtype...]
where the time goes in v3:
time: 33.8 us; the launch traced here: 33.6 us
  Pallas kernels  32.8 us (97%)
  local copies, waits for them, and re-layouts  0.8 us (2%)
    pallas_call x1, Pallas kernels, body(): pl.pallas_call(functools.partial(kernel, sizes), out_shape=jax.ShapeDtype...  32.8 us
    unnamed x1, local copies, waits for them, and re-layouts  0.8 us

profile of v3, /device:TPU:0, one launch (start us, length us, event | category | flops | bytes accessed | tf_op | source)
XLA Modules:
  0.0 33.6 jit_solution(18417488612753332556)
XLA Ops:
  0.0 32.8 %shard_map.28 = f32[1024,128]{1,0:T(8,128)S(1)} custom-call(f32[1024,128]{1,0:T(8,128)} %bitcast.3, s32[2,4,256]{2,1,0:T(4,128)} %plan_hbm.1), custom_call_target="tpu_custom_call" | custom-call | tf_op jit(solution)/shard_map/pallas_call | solution.py:391
  32.8 0.8 %copy.4 = f32[64,8,2,128]{3,2,1,0:T(2,128)} copy(f32[64,8,2,128]{3,2,1,0:T(2,128)S(1)} %bitcast.2) | data formatting | bytes 1048576

commit v4 on v2

--- a/solution.py
+++ b/solution.py
@@ -76,7 +76,7 @@
     sign = jnp.where(spread >= 0.0, 1.0, -1.0)
     root = jnp.sqrt(spread * spread + 4.0 * cross * cross)
     tangent = sign * 2.0 * cross / (jnp.abs(spread) + root)
-    cosine = 1.0 / jnp.sqrt(1.0 + tangent * tangent)
+    cosine = lax.rsqrt(1.0 + tangent * tangent)
     return cosine, tangent * cosine
 
 
@@ -107,8 +107,8 @@
 
 
 def kernel(sizes, x_hbm, plan_hbm, out_ref, x_ref, plan_ref, stage, held, state, bottoms, landed, tops, row_state,
-           row_tops, row_low, row_landed, turns, moves, sources, grams, load_sem, in_send, in_recv, mid_send, mid_recv,
-           gram_send, gram_recv, turn_send, turn_recv, row_send, row_recv):
+           row_tops, row_low, row_landed, turns, moves, sources, grams, clear, load_sem, in_send, in_recv, mid_send, mid_recv,
+           gram_send, gram_recv, turn_send, turn_recv, row_send, row_recv, direct):
     owners, groups, cols, rows_here, steps, rounds, width = sizes
     half = width // 2
     rows_all = owners * rows_here
@@ -140,28 +140,58 @@
     def rows_of(owner):
         return pl.ds(pl.multiple_of(owner * rows_here, rows_here), rows_here)
 
-    incoming = []
-    for d in range(1, owners):
-        copy = pltpu.make_async_remote_copy(
-            stage.at[(mine + d) % owners], held.at[rows_of(mine), :], in_send.at[0], in_recv.at[d],
+    incoming = {}
+    order = sorted(range(1, owners), key=lambda d: (abs(d - owners // 2), d))
+    first = owners - 6
+    for i, d in enumerate(order):
+        incoming[d] = pltpu.make_async_remote_copy(
+            stage.at[(mine + d) % owners], held.at[rows_of(mine), :], in_send.at[int(i + 1 >= first)], in_recv.at[d],
             device_id=at(d), device_id_type=MESH)
-        copy.start()
-        incoming.append(copy)
-
+
+    def send_rows():
+        for d in order:
+            incoming[d].start()
+
+    def rows_sent(slot, count):
+        sent = stage.at[0:count]
+        pltpu.make_async_remote_copy(
+            sent, sent, in_send.at[slot], in_recv.at[0], device_id=at(1), device_id_type=MESH).wait_send()
+
+    early = col % 2 == 1
+    pl.when(early)(send_rows)
     load_plan.wait()
-    with jax.named_scope("orders"):
-        ladder = lax.broadcasted_iota(jnp.int32, (8, width), 1).astype(F32).astype(BF16)
-        for s in range(steps):
-            before = None
-            for r in range(rounds + 1):
-                if r < rounds:
-                    forward, backward = orders(plan_ref[s, r:r + 1, :])
-                    move = forward if r == 0 else dot(before, forward).astype(BF16)
-                    before = backward
-                else:
-                    move = before
-                moves[s, r] = move
-                sources[s, r] = dot(ladder, move).astype(jnp.int32)
+    ladder = lax.broadcasted_iota(jnp.int32, (8, width), 1).astype(F32).astype(BF16)
+
+    def arrange(s):
+        before = None
+        for r in range(rounds + 1):
+            if r < rounds:
+                forward, backward = orders(plan_ref[s, r:r + 1, :])
+                move = forward if r == 0 else dot(before, forward).astype(BF16)
+                before = backward
+            else:
+                move = before
+            moves[s, r] = move
+            sources[s, r] = dot(ladder, move).astype(jnp.int32)
+
+    with jax.named_scope("orders0"):
+        arrange(0)
+
+    with jax.named_scope("hand_over"):
+        @pl.when(early)
+        def _():
+            rows_sent(0, first - 1)
+            partner = (me, (col + cols - 1) % cols)
+            pl.semaphore_signal(clear.at[0], inc=1, device_id=partner, device_id_type=MESH)
+
+        @pl.when(jnp.logical_not(early))
+        def _():
+            pl.semaphore_wait(clear.at[0], 1)
+            send_rows()
+
+    with jax.named_scope("orders1"):
+        for s in range(1, steps):
+            arrange(s)
 
     def advanced(ref, turn, s, r):
         parts = []
@@ -241,8 +271,14 @@
             return advanced(tops, turn, s, rounds)
         return advanced(state, all_turns[-1], s, rounds)
 
-    chunks = 2 if owners % 2 == 0 else 1
+    chunks = 2
     size = owners // chunks
+    side = mine // size
+
+    def near_landed(s, count):
+        block = row_landed.at[s, 0:count]
+        return pltpu.make_async_remote_copy(
+            block, block, direct.at[0, s], direct.at[1, s], device_id=(me, right), device_id_type=MESH)
 
     def short_moved(q, rows, s, r):
         flat = rows.reshape(size * rows_here, width)
@@ -268,39 +304,53 @@
     with jax.named_scope("a2a_wait"):
         held[rows_of(mine), :] = stage[mine]
         sums = first_step(rows_of(mine))
-        for d in range(1, owners):
-            incoming[d - 1].wait_recv()
+        for d in reversed(order):
+            incoming[d].wait_recv()
             more = first_step(rows_of((mine + owners - d) % owners))
             if more is not None:
                 sums = tuple(a + b for a, b in zip(sums, more))
 
-    passing = []
-    for s in range(steps):
+    cut = rows_all // 2
+
+    def crossing(s, h):
+        return pltpu.make_async_remote_copy(
+            bottoms.at[s, h], landed.at[s, h], mid_send.at[s, h], mid_recv.at[s, h],
+            device_id=(me, right), device_id_type=MESH)
+
+    def passing(s, q=0):
+        part = slice(q * size, (q + 1) * size)
+        return pltpu.make_async_remote_copy(
+            row_low.at[s, part], row_landed.at[s, part], row_send.at[s], row_recv.at[s],
+            device_id=(me, right), device_id_type=MESH)
+
+    def solve(s, sums):
         last = s + 1 == steps
         with jax.named_scope(f"solve{s}"):
             all_turns = solved(s, sums)
-        if not last:
-            with jax.named_scope(f"cross_send{s}"):
-                parts = final_parts(s, all_turns)
-                cut = rows_all // 2
-                crossing = []
-                for h in range(2):
-                    bottoms[s, h] = parts[h][:, half:]
-                    copy = pltpu.make_async_remote_copy(
-                        bottoms.at[s, h], landed.at[s, h], mid_send.at[s, h], mid_recv.at[s, h],
-                        device_id=(me, right), device_id_type=MESH)
-                    copy.start()
-                    crossing.append(copy)
-                    tops[h * cut:(h + 1) * cut, :half] = parts[h][:, :half]
+        with jax.named_scope(f"send{s}"):
+            parts = final_parts(s, all_turns)
+            for h in range(2):
+                bottoms[s, h] = parts[h][:, half:]
+                if last:
+                    continue
+                crossing(s, h).start()
+                tops[h * cut:(h + 1) * cut, :half] = parts[h][:, :half]
+            for j in range(0 if last else 1, size):
+                other = (mine + j) % size
+                pltpu.make_async_remote_copy(
+                    bottoms.at[s, side, rows_of(other), :], row_landed.at[s, mine], direct.at[0, s], direct.at[1, s],
+                    device_id=(group * owners + side * size + other, right), device_id_type=MESH).start()
+
+    def rows_step(s):
+        last = s + 1 == steps
         if s > 0:
             with jax.named_scope(f"pass_wait{s}"):
-                for copy in passing:
-                    copy.wait()
+                near_landed(s - 1, size - 1).wait()
+                passing(s - 1).wait()
             for q in range(chunks):
                 part = slice(q * size, (q + 1) * size)
                 rows = jnp.concatenate([row_tops[s - 1, part], row_landed[s - 1, part]], axis=2)
                 row_state[part] = short_moved(q, rows, s, 0)
-        passing = []
         for r in range(rounds):
             with jax.named_scope(f"told{s}_{r}"):
                 all_told(s, r).wait_recv()
@@ -316,39 +366,60 @@
                         row_state[part] = turned[q]
                         continue
                     row_low[s, part] = turned[q][:, :, half:]
-                    copy = pltpu.make_async_remote_copy(
-                        row_low.at[s, part], row_landed.at[s, part], row_send.at[s, q], row_recv.at[s, q],
-                        device_id=(me, right), device_id_type=MESH)
-                    copy.start()
-                    passing.append(copy)
+                    pl.when(side != q)(passing(s, q).start)
                     if last:
                         for k in range(size):
                             at_rows = pl.ds(2 * (q * size + k), rows_here, stride=2 * owners)
                             out_ref[at_rows, :] = turned[q][k, :, :half]
                     else:
                         row_tops[s, part] = turned[q][:, :, :half]
-        if not last:
-            sums = None
-            with jax.named_scope(f"cross_wait{s}"):
-                for copy in crossing:
-                    copy.wait()
-            with jax.named_scope(f"cross_join{s}"):
-                for h in range(2):
-                    tops[h * cut:(h + 1) * cut, half:] = landed[s, h]
-                if groups == 1:
-                    parts = advanced(tops, None, s + 1, 0)
-                    kept(state, parts)
-                    sums = products([(part, part) for part in parts])
+
+    def join(s):
+        with jax.named_scope(f"cross_wait{s}"):
+            for h in range(2):
+                crossing(s, h).wait()
+        with jax.named_scope(f"cross_join{s}"):
+            for h in range(2):
+                tops[h * cut:(h + 1) * cut, half:] = landed[s, h]
+            row_landed[s, mine] = landed[s, side, rows_of(mine % size), :]
+            if groups > 1:
+                return None
+            parts = advanced(tops, None, s + 1, 0)
+            kept(state, parts)
+            return products([(part, part) for part in parts])
+
+    solve(0, sums)
+    ahead = col % 2 == 0
+    for s in range(steps - 1):
+        @pl.when(ahead)
+        def _():
+            solve(s + 1, join(s))
+            rows_step(s)
+
+        @pl.when(jnp.logical_not(ahead))
+        def _():
+            rows_step(s)
+            solve(s + 1, join(s))
+
+    rows_step(steps - 1)
 
     for s in range(steps):
         all_tells(s).wait_send()
-    sent = stage.at[0:owners - 1]
-    pltpu.make_async_remote_copy(sent, sent, in_send.at[0], in_recv.at[0], device_id=at(1), device_id_type=MESH).wait_send()
-    for q in range(chunks):
-        with jax.named_scope("last_pass"):
-            passing[q].wait()
+    pl.when(jnp.logical_not(early))(functools.partial(rows_sent, 0, first - 1))
+    rows_sent(1, owners - first)
+
+    def put_bottoms(q):
         for k in range(q * size, (q + 1) * size):
             out_ref[pl.ds(2 * k + 1, rows_here, stride=2 * owners), :] = row_landed[steps - 1, k]
+
+    with jax.named_scope("direct_wait"):
+        near_landed(steps - 1, size).wait()
+    for q in range(chunks):
+        pl.when(side == q)(functools.partial(put_bottoms, q))
+    with jax.named_scope("last_pass"):
+        passing(steps - 1).wait()
+    for q in range(chunks):
+        pl.when(side != q)(functools.partial(put_bottoms, q))
 
 
 def body(mesh_sizes, matrix, plan):
@@ -356,7 +427,7 @@
     steps, rounds, width = plan.shape
     rows, cols = mesh_sizes
     owners, groups = pair_here, rows // pair_here
-    assert rows % pair_here == 0 and halves == 2 and cols > 1
+    assert rows % pair_here == 0 and pair_here % 2 == 0 and halves == 2 and cols > 1 and cols % 2 == 0
     sizes = (owners, groups, cols, rows_here, steps, rounds, width)
     dma = pltpu.SemaphoreType.DMA
     rows_all = owners * rows_here
@@ -374,7 +445,7 @@
             pltpu.VMEM((owners, rows_here, width), F32),
             pltpu.VMEM((rows_all, width), F32),
             pltpu.VMEM((rows_all if groups == 1 else 2 * width, width), F32),
-            pltpu.VMEM((steps - 1, 2, rows_all // 2, half), F32),
+            pltpu.VMEM((steps, 2, rows_all // 2, half), F32),
             pltpu.VMEM((steps - 1, 2, rows_all // 2, half), F32),
             pltpu.VMEM((rows_all, width), F32),
             pltpu.VMEM((owners, rows_here, width), F32),
@@ -385,9 +456,9 @@
             pltpu.VMEM((steps, rounds + 1, width, width), BF16),
             pltpu.VMEM((steps, rounds + 1, 8, width), jnp.int32),
             pltpu.VMEM((steps, groups, width, width) if groups > 1 else (1, 1, 8, 128), F32),
-            dma((2,)), dma((1,)), dma((owners,)), dma((steps - 1, 2)), dma((steps - 1, 2)),
+            pltpu.SemaphoreType.REGULAR((1,)), dma((2,)), dma((2,)), dma((owners,)), dma((steps - 1, 2)), dma((steps - 1, 2)),
             dma((steps, groups) if groups > 1 else (1, 1)), dma((steps, groups) if groups > 1 else (1, 1)),
-            dma((steps,)), dma((steps, rounds)), dma((steps, 2)), dma((steps, 2)),
+            dma((steps,)), dma((steps, rounds)), dma((steps,)), dma((steps,)), dma((2, steps)),
         ],
         compiler_params=pltpu.CompilerParams(collective_id=0, has_side_effects=True, vmem_limit_bytes=40 << 20),
     )(pltpu.with_memory_space_constraint(matrix.reshape(flat), pltpu.HBM),

time: 35 us -> 33 us (0.943)
  Pallas kernels: 34 us -> 32.1 us
    pallas_call x1, Pallas kernels: 34 us -> 32.1 us  [body(): pl.pallas_call(functools.partial(kernel, sizes), out_shape=jax.ShapeDtype...]
where the time goes in v4:
time: 33 us; the launch traced here: 32.9 us
  Pallas kernels  32.1 us (97%)
  local copies, waits for them, and re-layouts  0.8 us (2%)
    pallas_call x1, Pallas kernels, body(): pl.pallas_call(functools.partial(kernel, sizes), out_shape=jax.ShapeDtype...  32.1 us
    unnamed x1, local copies, waits for them, and re-layouts  0.8 us

profile of v4, /device:TPU:0, one launch (start us, length us, event | category | flops | bytes accessed | tf_op | source)
XLA Modules:
  0.0 32.9 jit_solution(15216820207908096060)
XLA Ops:
  0.0 32.1 %shard_map.28 = f32[1024,128]{1,0:T(8,128)S(1)} custom-call(f32[1024,128]{1,0:T(8,128)} %bitcast.3, s32[2,4,256]{2,1,0:T(4,128)} %plan_hbm.1), custom_call_target="tpu_custom_call" | custom-call | tf_op jit(solution)/shard_map/pallas_call | solution.py:437
  32.1 0.8 %copy.4 = f32[64,8,2,128]{3,2,1,0:T(2,128)} copy(f32[64,8,2,128]{3,2,1,0:T(2,128)S(1)} %bitcast.2) | data formatting | bytes 1048576

commit v5 on v4

--- a/solution.py
+++ b/solution.py
@@ -367,6 +367,8 @@
                         continue
                     row_low[s, part] = turned[q][:, :, half:]
                     pl.when(side != q)(passing(s, q).start)
+                for q in range(chunks if r + 1 == rounds else 0):
+                    part = slice(q * size, (q + 1) * size)
                     if last:
                         for k in range(size):
                             at_rows = pl.ds(2 * (q * size + k), rows_here, stride=2 * owners)

time: 33 us -> 33 us (level)
  no operation moved by 1% of the time
where the time goes in v5:
time: 33 us; the launch traced here: 32.8 us
  Pallas kernels  32 us (97%)
  local copies, waits for them, and re-layouts  0.8 us (2%)
    pallas_call x1, Pallas kernels, body(): pl.pallas_call(functools.partial(kernel, sizes), out_shape=jax.ShapeDtype...  32 us
    unnamed x1, local copies, waits for them, and re-layouts  0.8 us

profile of v5, /device:TPU:0, one launch (start us, length us, event | category | flops | bytes accessed | tf_op | source)
XLA Modules:
  0.0 32.8 jit_solution(6549370953872711481)
XLA Ops:
  0.0 32.0 %shard_map.28 = f32[1024,128]{1,0:T(8,128)S(1)} custom-call(f32[1024,128]{1,0:T(8,128)} %bitcast.3, s32[2,4,256]{2,1,0:T(4,128)} %plan_hbm.1), custom_call_target="tpu_custom_call" | custom-call | tf_op jit(solution)/shard_map/pallas_call | solution.py:439
  32.0 0.8 %copy.4 = f32[64,8,2,128]{3,2,1,0:T(2,128)} copy(f32[64,8,2,128]{3,2,1,0:T(2,128)S(1)} %bitcast.2) | data formatting | bytes 1048576

commit v6 on v5

--- a/solution.py
+++ b/solution.py
@@ -365,8 +365,12 @@
                     if r + 1 < rounds:
                         row_state[part] = turned[q]
                         continue
-                    row_low[s, part] = turned[q][:, :, half:]
-                    pl.when(side != q)(passing(s, q).start)
+
+                    @pl.when(side != q)
+                    def _():
+                        row_low[s, part] = turned[q][:, :, half:]
+                        passing(s, q).start()
+
                 for q in range(chunks if r + 1 == rounds else 0):
                     part = slice(q * size, (q + 1) * size)
                     if last:

time: 33 us -> 33 us (level)
  no operation moved by 1% of the time
where the time goes in v6:
time: 33 us; the launch traced here: 32.8 us
  Pallas kernels  32 us (97%)
  local copies, waits for them, and re-layouts  0.8 us (2%)
    pallas_call x1, Pallas kernels, body(): pl.pallas_call(functools.partial(kernel, sizes), out_shape=jax.ShapeDtype...  32 us
    unnamed x1, local copies, waits for them, and re-layouts  0.8 us

profile of v6, /device:TPU:0, one launch (start us, length us, event | category | flops | bytes accessed | tf_op | source)
XLA Modules:
  0.0 32.8 jit_solution(5348556499212265373)
XLA Ops:
  0.0 32.0 %shard_map.28 = f32[1024,128]{1,0:T(8,128)S(1)} custom-call(f32[1024,128]{1,0:T(8,128)} %bitcast.3, s32[2,4,256]{2,1,0:T(4,128)} %plan_hbm.1), custom_call_target="tpu_custom_call" | custom-call | tf_op jit(solution)/shard_map/pallas_call | solution.py:443
  32.0 0.8 %copy.4 = f32[64,8,2,128]{3,2,1,0:T(2,128)} copy(f32[64,8,2,128]{3,2,1,0:T(2,128)S(1)} %bitcast.2) | data formatting | bytes 1048576
